TPU v7x, 32 devices: a whole 2x2x4 slice. The times are simulated.
32 devices in a mesh: replica: 8 (over z, y), model: 4 (over x, core).
Axes of the slice: x: 2, y: 2, z: 4, core: 2. Of those that a mesh axis runs over, the one named last changes fastest.
Arguments:
- partial_up: float32 [8, 1024, 4096], P('replica', None, 'model'), may hold values from -4 to 4
- partial_down: float32 [8, 4096, 1024], P('replica', 'model'), may hold values from -4 to 4
- partial_norm: float32 [8, 1024], P('replica'), may hold values from -8 to 8
- partial_bias: float32 [8, 1024], P('replica'), may hold values from -8 to 8
- master_up: float32 [1024, 4096], P('replica', 'model'), may hold values from -0.1875 to 0.1875
- master_down: float32 [4096, 1024], P('model', 'replica'), may hold values from -0.09375 to 0.09375
- master_norm: float32 [1024], P('replica'), may hold values from 0.25 to 1.75
- master_bias: float32 [1024], P('replica'), may hold values from -3 to 3
- memory_up: float32 [1024, 4096], P('replica', 'model'), may hold values from 0.05 to 0.8
- memory_down: float32 [4096, 1024], P('model', 'replica'), may hold values from 0.05 to 0.8
- memory_norm: float32 [1024], P('replica'), may hold values from 0.05 to 0.8
- memory_bias: float32 [1024], P('replica'), may hold values from 0.05 to 0.8
Outputs:
- compute_up: bfloat16 [1024, 4096], P(None, 'model')
- compute_down: bfloat16 [4096, 1024], P('model')
- compute_norm: bfloat16 [1024], replicated
- compute_bias: bfloat16 [1024], replicated
- stepped_up: float32 [1024, 4096], P('replica', 'model')
- stepped_down: float32 [4096, 1024], P('model', 'replica')
- stepped_norm: float32 [1024], P('replica')
- stepped_bias: float32 [1024], P('replica')
- state_new_up: float32 [1024, 4096], P('replica', 'model')
- state_new_down: float32 [4096, 1024], P('model', 'replica')
- state_new_norm: float32 [1024], P('replica')
- state_new_bias: float32 [1024], P('replica')
All inputs are finite; a program needn't handle non-finite values.
Results may differ from a plain program's by a relative error of at most 0.001.
Values may be sent and summed in bfloat16 or wider, within the bound.
A program may use at most 128 MiB of HBM per device.

v0:
```python
import functools
import math

import jax
import jax.numpy as jnp
from jax import lax
from jax.experimental import pallas as pl
from jax.experimental.pallas import tpu as pltpu
from jax.sharding import PartitionSpec as P

learn_rate = 0.05
hold_rate = 0.9


def plain(
    partial_up,
    partial_down,
    partial_norm,
    partial_bias,
    master_up,
    master_down,
    master_norm,
    master_bias,
    memory_up,
    memory_down,
    memory_norm,
    memory_bias,
):
    mean_up, mean_down = (
        lax.psum_scatter(partial_up[0], "replica", scatter_dimension=0, tiled=True),
        lax.psum_scatter(partial_down[0], "replica", scatter_dimension=1, tiled=True),
    )
    whole_norm, whole_bias = lax.psum((partial_norm[0], partial_bias[0]), "replica")
    place = lax.axis_index("replica")
    mean_norm = lax.dynamic_slice_in_dim(
        whole_norm, place * master_norm.shape[0], master_norm.shape[0]
    )
    mean_bias = lax.dynamic_slice_in_dim(
        whole_bias, place * master_bias.shape[0], master_bias.shape[0]
    )
    mean_rate = lax.axis_size("replica") ** (-0.5)
    mean_up = mean_up * mean_rate
    mean_down = mean_down * mean_rate
    mean_norm = mean_norm * mean_rate
    mean_bias = mean_bias * mean_rate
    state_new_up = hold_rate * memory_up + (1.0 - hold_rate) * mean_up * mean_up
    stepped_up = master_up - learn_rate * mean_up * lax.rsqrt(state_new_up + 1e-06)
    state_new_down = hold_rate * memory_down + (1.0 - hold_rate) * mean_down * mean_down
    stepped_down = master_down - learn_rate * mean_down * lax.rsqrt(state_new_down + 1e-06)
    state_new_norm = hold_rate * memory_norm + (1.0 - hold_rate) * mean_norm * mean_norm
    stepped_norm = master_norm - learn_rate * mean_norm * lax.rsqrt(state_new_norm + 1e-06)
    state_new_bias = hold_rate * memory_bias + (1.0 - hold_rate) * mean_bias * mean_bias
    stepped_bias = master_bias - learn_rate * mean_bias * lax.rsqrt(state_new_bias + 1e-06)
    compute_up, compute_down, compute_norm, compute_bias = (
        lax.all_gather(stepped_up.astype(jnp.bfloat16), "replica", axis=0, tiled=True),
        lax.all_gather(stepped_down.astype(jnp.bfloat16), "replica", axis=1, tiled=True),
        lax.all_gather(stepped_norm.astype(jnp.bfloat16), "replica", axis=0, tiled=True),
        lax.all_gather(stepped_bias.astype(jnp.bfloat16), "replica", axis=0, tiled=True),
    )
    return (
        compute_up,
        compute_down,
        compute_norm,
        compute_bias,
        stepped_up,
        stepped_down,
        stepped_norm,
        stepped_bias,
        state_new_up,
        state_new_down,
        state_new_norm,
        state_new_bias,
    )


CHUNKS = 8
STEEP = 32.0
SPAN = 124.0
POWER = 2.0 * SPAN / math.log1p(STEEP)


def encode(x, reach):
    y = jnp.exp2(POWER * jnp.log(1.0 + jnp.abs(x) * (STEEP / reach)) - SPAN)
    return jnp.where(x < 0.0, -y, y).astype(jnp.bfloat16)


def decode(code, reach):
    y = code.astype(jnp.float32)
    grown = jnp.exp2((jnp.log(jnp.abs(y)) * (1.0 / math.log(2.0)) + SPAN) * (math.log1p(STEEP) / (2.0 * SPAN * math.log(2.0))))
    x = (grown - 1.0) * (reach / STEEP)
    return jnp.where(y < 0.0, -x, x)


def update(total, master, memory, rate):
    mean = total * rate
    state = hold_rate * memory + (1.0 - hold_rate) * mean * mean
    return master - learn_rate * mean * lax.rsqrt(state + 1e-06), state


def kernel(
    n,
    pu, pd, mu, md, su, sd, pn, pb, mn, mb, sn, sb,
    gu, gd, ou, od, qu, qd, cn, cb, step_s, state_s,
    xu, xd, wu, wd, hu, hd,
    au, ad, ru, rd, bu, bd, zu, zd,
    mine, theirs, hold_s,
    sem_in, sem_par, sem_vec, sem_as, sem_ar, sem_bs, sem_br, sem_ds, sem_dr, sem_es, sem_er,
    sem_vs, sem_vr,
):
    K = CHUNKS
    nz = n // 2
    me = lax.axis_index("replica")
    y = lax.rem(me, 2)
    z = lax.div(me, 2)
    other = me + 1 - 2 * y
    rate = n ** (-0.5)
    reach = n / 2.0
    wide = 128
    hr = xu.shape[1] // K
    rr = xd.shape[0] // K

    def up_z(d):
        return lax.rem(z + d, nz)

    def from_z(d):
        return lax.rem(z + nz - d, nz)

    def remote(src, dst, ss, rs, who):
        return pltpu.make_async_remote_copy(
            src_ref=src, dst_ref=dst, send_sem=ss, recv_sem=rs,
            device_id={"replica": who}, device_id_type=pl.DeviceIdType.MESH,
        )

    def rows(k, h):
        return pl.ds(pl.multiple_of(k * h, h), h)

    def lanes(b):
        return pl.ds(pl.multiple_of(b * wide, wide), wide)

    def load_in(m, k):
        if m == 0:
            return pltpu.make_async_copy(pu.at[:, rows(k, hr), :], xu.at[:, rows(k, hr), :], sem_in.at[m, k])
        return pltpu.make_async_copy(pd.at[rows(k, rr), :], xd.at[rows(k, rr), :], sem_in.at[m, k])

    def block(m, k, b):
        if m == 0:
            return xu[b, rows(k, hr), :]
        return xd[rows(k, rr), lanes(b)]

    def span(m, k):
        return rows(k, (hr, rr)[m])

    asend, arecv, bsend, brecv, gath = (au, ad), (ru, rd), (bu, bd), (zu, zd), (gu, gd)

    def copy_a(m, k):
        return remote(asend[m].at[k], arecv[m].at[k], sem_as.at[m, k], sem_ar.at[m, k], other)

    def copy_b(m, k, d):
        return remote(
            bsend[m].at[k, up_z(d)], brecv[m].at[k, d - 1],
            sem_bs.at[m, k, d - 1], sem_br.at[m, k, d - 1], 2 * up_z(d) + y,
        )

    def inside(t):
        return jnp.logical_and(t >= 0, t < nz)

    def copy_d(m, k, way, d):
        step = (1, -1)[way]
        piece = gath[m].at[2 * (z - step * d) + y, span(m, k), :]
        at = way * (nz - 1) + d
        return remote(piece, piece, sem_ds.at[m, k, at], sem_dr.at[m, k, at], 2 * (z + step) + y)

    def landed_d(m, k, way, d):
        piece = gath[m].at[2 * (z - (1, -1)[way] * d) + y, span(m, k), :]
        at = way * (nz - 1) + d - 1
        return remote(piece, piece, sem_ds.at[m, k, at], sem_dr.at[m, k, at], other)

    def sends(way, d):
        step = (1, -1)[way]
        return jnp.logical_and(inside(z - step * d), inside(z + step))

    def copy_e(m, k, t):
        piece = gath[m].at[2 * t + y, span(m, k), :]
        return remote(piece, piece, sem_es.at[m, k, t], sem_er.at[m, k, t], other)

    def copy_v(d):
        return remote(mine, theirs.at[d - 1], sem_vs.at[d - 1], sem_vr.at[d - 1], lax.rem(me + d, n))

    def each(m, body):
        lax.fori_loop(0, K, lambda k, c: (body(m, k), c)[1], 0)

    params = [
        pltpu.make_async_copy(a, b, sem_par.at[i])
        for i, (a, b) in enumerate(((mu, wu), (md, wd), (su, hu), (sd, hd)))
    ]
    each(0, lambda m, k: load_in(m, k).start())
    each(1, lambda m, k: load_in(m, k).start())
    for p in params:
        p.start()

    vectors = [
        pltpu.make_async_copy(a, mine.at[at : at + a.shape[0], :], sem_vec.at[i])
        for i, (a, at) in enumerate(
            ((pn, 0), (pb, n), (mn, 2 * n), (mb, 2 * n + 1), (sn, 2 * n + 2), (sb, 2 * n + 3))
        )
    ]
    mine[2 * n + 4 : 2 * n + 8, :] = jnp.zeros((4, wide), jnp.float32)
    for p in vectors:
        p.start()

    barrier = pltpu.get_barrier_semaphore()
    for d in range(1, n):
        pl.semaphore_signal(
            barrier, inc=1, device_id={"replica": lax.rem(me + d, n)},
            device_id_type=pl.DeviceIdType.MESH,
        )

    def encode_a(m, k):
        load_in(m, k).wait()

        def one(t, c):
            asend[m][k, t] = encode(block(m, k, 2 * t + 1 - y), reach)
            return c

        lax.fori_loop(0, nz, one, 0)

    def phase_a(m, k):
        encode_a(m, k)
        copy_a(m, k).start()

    def phase_b(m, k):
        copy_a(m, k).wait_recv()

        def one(t, c):
            pair = block(m, k, 2 * t + y) + decode(arecv[m][k, t], reach)
            bsend[m][k, t] = encode(pair, 2.0 * reach)
            return c

        lax.fori_loop(0, nz, one, 0)
        for d in range(1, nz):
            copy_b(m, k, d).start()

    def phase_c(m, k):
        for d in range(1, nz):
            copy_b(m, k, d).wait_recv()
        total = block(m, k, me) + decode(arecv[m][k, z], reach)
        for d in range(1, nz):
            total = total + decode(brecv[m][k, d - 1], 2.0 * reach)
        master, memory = ((wu, wd)[m], (hu, hd)[m])
        stepped, state = update(total, master[span(m, k), :], memory[span(m, k), :], rate)
        (ou, od)[m][span(m, k), :] = stepped
        (qu, qd)[m][span(m, k), :] = state
        gath[m][me, span(m, k), :] = stepped.astype(jnp.bfloat16)
        copy_e(m, k, z).start()
        for way in range(2):

            @pl.when(sends(way, 0))
            def _():
                copy_d(m, k, way, 0).start()


    def phase_d(m, k, d):
        for way in range(2):
            origin = z - (1, -1)[way] * d

            @pl.when(inside(origin))
            def _():
                landed_d(m, k, way, d).wait_recv()
                copy_e(m, k, origin).start()

            if d < nz - 1:

                @pl.when(sends(way, d))
                def _():
                    copy_d(m, k, way, d).start()

    def phase_e(m, k):
        for d in range(nz):
            copy_e(m, k, d).wait_recv()

    pl.semaphore_wait(barrier, n - 1)
    each(0, phase_a)
    each(1, phase_a)
    for p in vectors:
        p.wait()
    for d in range(1, n):
        copy_v(d).start()
    each(0, phase_b)
    for p in params:
        p.wait()

    def phase_bc(m, k):
        phase_b(1, k)
        phase_c(0, k)

    each(0, phase_bc)
    each(1, phase_c)

    for d in range(1, n):
        copy_v(d).wait_recv()
    slot = lambda j: lax.rem(me - j + n - 1 + n, n)
    total = None
    for j in range(n):
        held = theirs[lax.rem(slot(j), n - 1)]
        part = jnp.where(me == j, mine[...], held)
        for i in range(4):
            hold_s[i * n + j : i * n + j + 1, :] = part[2 * n + i : 2 * n + i + 1, :]
        total = part[0 : 2 * n, :] if total is None else total + part[0 : 2 * n, :]
    stepped, state = update(total, hold_s[0 : 2 * n, :], hold_s[2 * n : 4 * n, :], rate)
    cn[...] = stepped[0:n].astype(jnp.bfloat16)
    cb[...] = stepped[n : 2 * n].astype(jnp.bfloat16)
    step_s[...] = stepped
    state_s[...] = state

    for d in range(1, nz):
        each(0, functools.partial(phase_d, d=d))
        each(1, functools.partial(phase_d, d=d))
    each(0, phase_e)
    each(1, phase_e)

    def drain(m, k):
        copy_a(m, k).wait_send()
        for d in range(1, nz):
            copy_b(m, k, d).wait_send()
            for way in range(2):

                @pl.when(sends(way, d - 1))
                def _():
                    copy_d(m, k, way, d - 1).wait_send()

        for d in range(nz):
            copy_e(m, k, d).wait_send()

    each(0, drain)
    each(1, drain)
    for d in range(1, n):
        copy_v(d).wait_send()


def leave(
    n, gu, gd, ou, od, qu, qd, cn, cb, step_s, state_s,
    cu, cd, tu, td, vu, vd, xcn, xcb, tn, tb, vn, vb, sem,
):
    me = lax.axis_index("replica")
    wide = gd.shape[2]
    pairs = [(gu, cu)]
    pairs += [(gd.at[b], cd.at[:, b * wide : (b + 1) * wide]) for b in range(n)]
    pairs += [(ou, tu), (od, td), (qu, vu), (qd, vd), (cn, xcn), (cb, xcb)]
    pairs += [(step_s.at[pl.ds(me, 1), :], tn), (step_s.at[pl.ds(me + n, 1), :], tb)]
    pairs += [(state_s.at[pl.ds(me, 1), :], vn), (state_s.at[pl.ds(me + n, 1), :], vb)]
    copies = [pltpu.make_async_copy(a, b, sem.at[i]) for i, (a, b) in enumerate(pairs)]
    for c in copies:
        c.start()
    for c in copies:
        c.wait()


def fused(
    n, partial_up, partial_down, partial_norm, partial_bias, master_up, master_down,
    master_norm, master_bias, memory_up, memory_down, memory_norm, memory_bias,
):
    K = CHUNKS
    nz = n // 2
    hb, w = master_up.shape
    rows, wide = master_down.shape
    hr, rr = hb // K, rows // K
    f32, b16 = jnp.float32, jnp.bfloat16
    line = lambda a: a.reshape(1, -1)
    operands = (
        partial_up[0].reshape(n, hb, w), partial_down[0], master_up, master_down,
        memory_up, memory_down, partial_norm.reshape(n, -1), partial_bias.reshape(n, -1),
        line(master_norm), line(master_bias), line(memory_norm), line(memory_bias),
    )
    S = jax.ShapeDtypeStruct
    shapes = (
        S((n, hb, w), b16), S((rows, n * wide), b16),
        S((hb, w), f32), S((rows, wide), f32), S((hb, w), f32), S((rows, wide), f32),
        S((n, wide), b16), S((n, wide), b16),
        S((1, wide), f32), S((1, wide), f32), S((1, wide), f32), S((1, wide), f32),
    )
    hbm = pl.BlockSpec(memory_space=pltpu.HBM)
    vm = pl.BlockSpec(memory_space=pltpu.VMEM)
    D = pltpu.SemaphoreType.DMA
    V = pltpu.VMEM
    held = pl.pallas_call(
        functools.partial(kernel, n),
        out_shape=(
            S((n, hb, w), b16), S((n, rows, wide), b16),
            S((hb, w), f32), S((rows, wide), f32), S((hb, w), f32), S((rows, wide), f32),
            S((n, wide), b16), S((n, wide), b16), S((2 * n, wide), f32), S((2 * n, wide), f32),
        ),
        in_specs=[hbm] * 12,
        out_specs=[vm] * 10,
        scratch_shapes=[
            V((n, hb, w), f32), V((rows, n * wide), f32),
            V((hb, w), f32), V((rows, wide), f32), V((hb, w), f32), V((rows, wide), f32),
            V((K, nz, hr, w), b16), V((K, nz, rr, wide), b16),
            V((K, nz, hr, w), b16), V((K, nz, rr, wide), b16),
            V((K, nz, hr, w), b16), V((K, nz, rr, wide), b16),
            V((K, nz - 1, hr, w), b16), V((K, nz - 1, rr, wide), b16),
            V((2 * n + 8, wide), f32), V((n - 1, 2 * n + 8, wide), f32), V((4 * n, wide), f32),
            D((2, K)), D((4,)), D((6,)), D((2, K)), D((2, K)), D((2, K, nz - 1)),
            D((2, K, nz - 1)), D((2, K, 2 * nz - 2)), D((2, K, 2 * nz - 2)), D((2, K, nz)),
            D((2, K, nz)), D((n - 1,)), D((n - 1,)),
        ],
        compiler_params=pltpu.CompilerParams(
            collective_id=0, has_side_effects=True, vmem_limit_bytes=40 * 1024 * 1024
        ),
    )(*[pltpu.with_memory_space_constraint(a, pltpu.HBM) for a in operands])
    cu, cd, tu, td, vu, vd, cn, cb, tn, tb, vn, vb = pl.pallas_call(
        functools.partial(leave, n),
        out_shape=shapes,
        in_specs=[vm] * 10,
        out_specs=[hbm] * 12,
        scratch_shapes=[D((n + 11,))],
        compiler_params=pltpu.CompilerParams(vmem_limit_bytes=4 * 1024 * 1024),
    )(*held)
    flat = lambda a: a.reshape(-1)
    return (
        cu.reshape(n * hb, w), cd, flat(cn), flat(cb),
        tu, td, flat(tn), flat(tb), vu, vd, flat(vn), flat(vb),
    )


def on_device(*args):
    n = lax.axis_size("replica")
    hb, rows, wide = args[4].shape[0], args[5].shape[0], args[5].shape[1]
    fits = n % 8 == 0 and wide == 128 and args[6].shape[0] == wide and args[7].shape[0] == wide
    fits = fits and hb % (16 * CHUNKS) == 0 and rows % (16 * CHUNKS) == 0 and n <= 16
    return fused(n, *args) if fits else plain(*args)


def solution(mesh):
    in_specs = (
        P("replica", None, "model"),
        P("replica", "model", None),
        P("replica", None),
        P("replica", None),
        P("replica", "model"),
        P("model", "replica"),
        P("replica"),
        P("replica"),
        P("replica", "model"),
        P("model", "replica"),
        P("replica"),
        P("replica"),
    )
    out_specs = (
        P(None, "model"),
        P("model", None),
        P(),
        P(),
        P("replica", "model"),
        P("model", "replica"),
        P("replica"),
        P("replica"),
        P("replica", "model"),
        P("model", "replica"),
        P("replica"),
        P("replica"),
    )
    return jax.shard_map(
        on_device, mesh=mesh, in_specs=in_specs, out_specs=out_specs, check_vma=False
    )
```

profile of v0, /device:TPU:0, one launch (start us, length us, event | category | flops | bytes accessed | tf_op | source)
XLA Modules:
  0.0 106.8 jit_solution(15277209894088173625)
XLA Ops:
  0.6 103.3 %shard_map.211 = (bf16[8,128,1024]{2,1,0:T(8,128)(2,1)S(1)}, bf16[8,1024,128]{2,1,0:T(8,128)(2,1)S(1)}, f32[128,1024]{1,0:T(8,128)S(1)}, f32[1024,128]{1,0:T(8,1...) custom-call(f32[8,128,1024]{2,1,0:T(8,128)} %bitcast.15, ...), custom_call_target="tpu_custom_call" | custom-call | tf_op jit(solution)/shard_map/pallas_call | solution.py:385
  103.9 2.8 %shard_map.212 = (bf16[8,128,1024]{2,1,0:T(8,128)(2,1)}, bf16[1024,1024]{1,0:T(8,128)(2,1)}, f32[128,1024]{1,0:T(8,128)}, f32[1024,128]{1,0:T(8,128)}, f32[128,1...) custom-call(bf16[8,128,1024]{2,1,0:T(8,128)(2,1)S(1)} %get-tuple-ele, ...), custom_call_target="tpu_custom_call" | custom-call | tf_op jit(solution)/shard_map/pallas_call | solution.py:410
where the time goes:
time: 107 us
  Pallas kernels  106 us (99%)
    pallas_call x1, Pallas kernels, fused(): pl.pallas_call(functools.partial(kernel, n), out_shape=(S((n, hb, w), b16...  103 us
    pallas_call x1, Pallas kernels, fused(): pl.pallas_call(functools.partial(leave, n), out_shape=shapes, in_specs=[v...  2.83 us

commit v1 on v0

v1 whole, which is shorter than its diff:
```python
import functools
import math

import jax
import jax.numpy as jnp
from jax import lax
from jax.experimental import pallas as pl
from jax.experimental.pallas import tpu as pltpu
from jax.sharding import PartitionSpec as P

learn_rate = 0.05
hold_rate = 0.9


def plain(
    partial_up,
    partial_down,
    partial_norm,
    partial_bias,
    master_up,
    master_down,
    master_norm,
    master_bias,
    memory_up,
    memory_down,
    memory_norm,
    memory_bias,
):
    mean_up, mean_down = (
        lax.psum_scatter(partial_up[0], "replica", scatter_dimension=0, tiled=True),
        lax.psum_scatter(partial_down[0], "replica", scatter_dimension=1, tiled=True),
    )
    whole_norm, whole_bias = lax.psum((partial_norm[0], partial_bias[0]), "replica")
    place = lax.axis_index("replica")
    mean_norm = lax.dynamic_slice_in_dim(
        whole_norm, place * master_norm.shape[0], master_norm.shape[0]
    )
    mean_bias = lax.dynamic_slice_in_dim(
        whole_bias, place * master_bias.shape[0], master_bias.shape[0]
    )
    mean_rate = lax.axis_size("replica") ** (-0.5)
    mean_up = mean_up * mean_rate
    mean_down = mean_down * mean_rate
    mean_norm = mean_norm * mean_rate
    mean_bias = mean_bias * mean_rate
    state_new_up = hold_rate * memory_up + (1.0 - hold_rate) * mean_up * mean_up
    stepped_up = master_up - learn_rate * mean_up * lax.rsqrt(state_new_up + 1e-06)
    state_new_down = hold_rate * memory_down + (1.0 - hold_rate) * mean_down * mean_down
    stepped_down = master_down - learn_rate * mean_down * lax.rsqrt(state_new_down + 1e-06)
    state_new_norm = hold_rate * memory_norm + (1.0 - hold_rate) * mean_norm * mean_norm
    stepped_norm = master_norm - learn_rate * mean_norm * lax.rsqrt(state_new_norm + 1e-06)
    state_new_bias = hold_rate * memory_bias + (1.0 - hold_rate) * mean_bias * mean_bias
    stepped_bias = master_bias - learn_rate * mean_bias * lax.rsqrt(state_new_bias + 1e-06)
    compute_up, compute_down, compute_norm, compute_bias = (
        lax.all_gather(stepped_up.astype(jnp.bfloat16), "replica", axis=0, tiled=True),
        lax.all_gather(stepped_down.astype(jnp.bfloat16), "replica", axis=1, tiled=True),
        lax.all_gather(stepped_norm.astype(jnp.bfloat16), "replica", axis=0, tiled=True),
        lax.all_gather(stepped_bias.astype(jnp.bfloat16), "replica", axis=0, tiled=True),
    )
    return (
        compute_up,
        compute_down,
        compute_norm,
        compute_bias,
        stepped_up,
        stepped_down,
        stepped_norm,
        stepped_bias,
        state_new_up,
        state_new_down,
        state_new_norm,
        state_new_bias,
    )


HALVES = 2
SHARE = 5 / 8
SPAN = 124.0
POWER = 49
STEEP = 2.0 ** (2.0 * SPAN / POWER) - 1.0
LOW = 2.0 ** (-SPAN / POWER)
LAG_PAIR = 4
LAG_SUM = 2
LAG_GATHER = 2
LAG_SIDE = 2
LAG_VECTOR = 4


def encode(x, reach):
    q = x * (LOW * STEEP / reach) + jnp.where(x < 0.0, -LOW, LOW)
    q2 = q * q
    q3 = q2 * q
    q6 = q3 * q3
    q12 = q6 * q6
    q24 = q12 * q12
    q48 = q24 * q24
    return (q48 * q).astype(jnp.bfloat16)


def decode(code, reach):
    y = code.astype(jnp.float32)
    grown = jnp.exp2(jnp.log(jnp.abs(y)) * (1.0 / (math.log(2.0) * POWER)))
    scale = reach / (LOW * STEEP)
    return (grown - LOW) * jnp.where(y < 0.0, -scale, scale)


def update(total, master, memory, rate):
    mean = total * rate
    state = hold_rate * memory + (1.0 - hold_rate) * mean * mean
    return master - learn_rate * mean * lax.rsqrt(state + 1e-06), state


def shares(hb):
    size = hb // HALVES
    first = int(size * SHARE) // 8 * 8
    return size, first, size - first


def kernel(
    n,
    pu, pd, mu, md, su, sd, pn, pb, mn, mb, sn, sb,
    gy, gz, ou, od, qu, qd, cn, cb, step_s, state_s,
    xs, wu, wd, hu, hd,
    a_s, a_r, c_s0, c_s1, c_r0, c_r1, z_s0, z_s1, z_r0, z_r1, y_s, y_r,
    mine, theirs, packs, hold_s,
    sem_up, sem_down, sem_par, sem_vec,
    sa, ra, sc, rc, sz, rz, sy, ry, so, ro, st, rt, sf, rf, sg, rg, sp, rp, sq, rq, sv, rv, sw, rw,
):
    H = HALVES
    nz = n // 2
    tiles, _, hb, wide = xs.shape
    size, part_y, part_z = shares(hb)
    tiles_up = pu.shape[2] // wide
    units = tiles * H
    me = lax.axis_index("replica")
    y = lax.rem(me, 2)
    row = lax.div(me, 2)
    other = me + 1 - 2 * y
    rate = n ** (-0.5)
    reach = n / 2.0
    c_s, c_r, z_s, z_r = (c_s0, c_s1), (c_r0, c_r1), (z_s0, z_s1), (z_r0, z_r1)

    def remote(src, dst, ss, rs, who):
        return pltpu.make_async_remote_copy(
            src_ref=src, dst_ref=dst, send_sem=ss, recv_sem=rs,
            device_id={"replica": who}, device_id_type=pl.DeviceIdType.MESH,
        )

    def load_up(k):
        lanes = pl.ds(pl.multiple_of(k * wide, wide), wide)
        return pltpu.make_async_copy(pu.at[:, :, lanes], xs.at[k], sem_up.at[k])

    def load_down(b):
        return pltpu.make_async_copy(
            pd.at[:, :, b * wide : (b + 1) * wide], xs.at[tiles_up:tiles, b], sem_down.at[b]
        )

    params = [
        pltpu.make_async_copy(a, b, sem_par.at[i])
        for i, (a, b) in enumerate(((mu, wu), (su, hu), (md, wd), (sd, hd)))
    ]
    vectors = [
        pltpu.make_async_copy(a, mine.at[at : at + a.shape[0], :], sem_vec.at[i])
        for i, (a, at) in enumerate(
            ((pn, 0), (pb, n), (mn, 2 * n), (mb, 2 * n + 1), (sn, 2 * n + 2), (sb, 2 * n + 3))
        )
    ]

    def tile_of(u):
        return lax.div(u, H), lax.rem(u, H)

    def rows_y(half):
        return pl.ds(pl.multiple_of(half * size, 8), part_y)

    def rows_z(half):
        return pl.ds(pl.multiple_of(half * size + part_y, 8), part_z)

    def encode_a(u):
        k, half = tile_of(u)

        @pl.when(jnp.logical_and(half == 0, k < tiles_up))
        def _():
            load_up(k).wait()

        @pl.when(u == tiles_up * H)
        def _():
            for b in range(n):
                load_down(b).wait()

        for t in range(nz):
            a_s[u, t] = encode(xs[k, 2 * t + 1 - y, rows_y(half), :], reach)

    load_up(0).start()
    barrier = pltpu.get_barrier_semaphore()
    pl.semaphore_signal(barrier, inc=1, device_id={"replica": other}, device_id_type=pl.DeviceIdType.MESH)

    @pl.when(row > 0)
    def _():
        pl.semaphore_signal(barrier, inc=1, device_id={"replica": me - 2}, device_id_type=pl.DeviceIdType.MESH)

    @pl.when(row < nz - 1)
    def _():
        pl.semaphore_signal(barrier, inc=1, device_id={"replica": me + 2}, device_id_type=pl.DeviceIdType.MESH)

    lax.fori_loop(1, tiles_up, lambda k, c: (load_up(k).start(), c)[1], 0)
    for p in params[:2]:
        p.start()
    mine[2 * n + 4 : 2 * n + 8, :] = jnp.zeros((4, wide), jnp.float32)
    for p in vectors:
        p.start()
    for b in range(n):
        load_down(b).start()
    for p in params[2:]:
        p.start()
    encode_a(jnp.int32(0))

    def run(z):
        poses = (z, nz - 1 - z)
        far = max(poses)
        pl.semaphore_wait(barrier, 1 + (z > 0) + (z < nz - 1))

        def beyond(d):
            return slice(z + 1, nz) if d == 0 else slice(0, z)

        def behind(d):
            return slice(0, z) if d == 0 else slice(z + 1, nz)

        def inward(d):
            return slice(z, nz) if d == 0 else slice(0, z + 1)

        def nextdev(d):
            return me + (2, -2)[d]

        def copy_a(u):
            return remote(a_s.at[u], a_r.at[u], sa.at[0], ra.at[u], other)

        def copy_c(u, d, sl):
            return remote(c_s[d].at[u, sl], c_r[d].at[u, sl], sc.at[d], rc.at[d, u], nextdev(d))

        def copy_z(u, d, sl):
            return remote(z_s[d].at[u, sl], z_r[d].at[u, sl], sz.at[d], rz.at[d, u], nextdev(d))

        def copy_y(u):
            return remote(y_s.at[u], y_r.at[u], sy.at[0], ry.at[u], other)

        def piece(ref, ss, rs, d, u):
            return remote(ref, ref, ss.at[d], rs.at[d, u], nextdev(d))

        def own_y(u, d, o):
            k, half = tile_of(u)
            return piece(gy.at[k, o, y, half], so, ro, d, u)

        def rest_y(u, d, sl):
            k, half = tile_of(u)
            return piece(gy.at[k, sl, y, half], st, rt, d, u)

        def fin_y(u):
            k, half = tile_of(u)
            ref = gy.at[k, :, y, half]
            return remote(ref, ref, sf.at[0], rf.at[0], other)

        def side_z(u, who):
            k, half = tile_of(u)
            ref = gz.at[k, z, who, half]
            return remote(ref, ref, sg.at[0], rg.at[u], other)

        def own_z(u, d, o):
            k, half = tile_of(u)
            return piece(gz.at[k, o, :, half], sp, rp, d, u)

        def rest_z(u, d, sl):
            k, half = tile_of(u)
            return piece(gz.at[k, sl, :, half], sq, rq, d, u)

        def prior(d):
            sl = behind(d)
            return z - 1 if d == 0 else z + 1, (slice(0, z - 1) if d == 0 else slice(z + 2, nz))

        def pair_y(u):
            k, half = tile_of(u)
            copy_a(u).wait_recv()
            for t in range(nz):
                at = (k, 2 * t + y, rows_y(half))
                xs[at] = xs[at] + decode(a_r[u, t], reach)

        def chain_y(u, d):
            k, half = tile_of(u)
            pos = poses[d]
            if pos > 0:
                copy_c(u, d, inward(d)).wait_recv()
            for t in range(nz)[beyond(d)]:
                value = xs[k, 2 * t + y, rows_y(half), :]
                if pos > 0:
                    value = value + decode(c_r[d][u, t], 2.0 * reach * pos)
                c_s[d][u, t] = encode(value, 2.0 * reach * (pos + 1))
            if pos < nz - 1:
                copy_c(u, d, beyond(d)).start()

        def finish(k, half, rows, count, total, put):
            at = pl.multiple_of(half * size, 8) + (0 if put is gy else part_y)

            @pl.when(k < tiles_up)
            def _():
                spot = (pl.ds(pl.multiple_of(at, 8), count), pl.ds(pl.multiple_of(k * wide, wide), wide))
                stepped, state = update(total, wu[spot], hu[spot], rate)
                ou[spot] = stepped
                qu[spot] = state
                put[k, z, y, half] = stepped.astype(jnp.bfloat16)

            @pl.when(k >= tiles_up)
            def _():
                spot = pl.ds(pl.multiple_of((k - tiles_up) * hb + at, 8), count)
                stepped, state = update(total, wd[spot, :], hd[spot, :], rate)
                od[spot, :] = stepped
                qd[spot, :] = state
                put[k, z, y, half] = stepped.astype(jnp.bfloat16)

        def close_y(u):
            k, half = tile_of(u)
            total = xs[k, me, rows_y(half), :]
            for d in range(2):
                if poses[d] > 0:
                    total = total + decode(c_r[d][u, z], 2.0 * reach * poses[d])
            finish(k, half, rows_y(half), part_y, total, gy)
            for d in range(2):
                if poses[d] < nz - 1:
                    own_y(u, d, z).start()

        def relay_y(u, d):
            pos = poses[d]
            o, sl = prior(d)
            own_y(u, d, o).wait_recv()
            if pos > 1:
                rest_y(u, d, sl).wait_recv()
            if pos < nz - 1:
                rest_y(u, d, behind(d)).start()

        def last_y(u):
            fin_y(u).start()

        def chain_z(u, d):
            k, half = tile_of(u)
            pos = poses[d]
            if pos > 0:
                copy_z(u, d, inward(d)).wait_recv()
            for t in range(nz)[beyond(d)]:
                for j in range(2):
                    value = xs[k, 2 * t + j, rows_z(half), :]
                    if pos > 0:
                        value = value + decode(z_r[d][u, t, j], reach * pos)
                    z_s[d][u, t, j] = encode(value, reach * (pos + 1))
            if pos < nz - 1:
                copy_z(u, d, beyond(d)).start()

        def cross_z(u):
            k, half = tile_of(u)
            sums = []
            for who in (1 - y, y):
                total = xs[k, 2 * z + who, rows_z(half), :]
                for d in range(2):
                    if poses[d] > 0:
                        total = total + decode(z_r[d][u, z, who], reach * poses[d])
                sums.append(total)
            y_s[u] = encode(sums[0], reach * nz)
            copy_y(u).start()
            xs[k, me, rows_z(half), :] = sums[1]

        def close_z(u):
            k, half = tile_of(u)
            copy_y(u).wait_recv()
            total = xs[k, me, rows_z(half), :] + decode(y_r[u], reach * nz)
            finish(k, half, rows_z(half), part_z, total, gz)
            side_z(u, y).start()

        def spread_z(u):
            side_z(u, 1 - y).wait_recv()
            for d in range(2):
                if poses[d] < nz - 1:
                    own_z(u, d, z).start()

        def relay_z(u, d):
            pos = poses[d]
            o, sl = prior(d)
            own_z(u, d, o).wait_recv()
            if pos > 1:
                rest_z(u, d, sl).wait_recv()
            if pos < nz - 1:
                rest_z(u, d, behind(d)).start()

        def vec_send():
            for p in vectors:
                p.wait()
            remote(mine, theirs, sv.at[0], rv.at[0], other).start()

        def vec_pair():
            remote(mine, theirs, sv.at[0], rv.at[0], other).wait_recv()
            a, b = mine[...], theirs[...]
            packs[z, 0 : 2 * n, :] = a[0 : 2 * n, :] + b[0 : 2 * n, :]
            first = y == 0
            packs[z, 2 * n : 2 * n + 8, :] = jnp.concatenate(
                [
                    jnp.where(first, a[2 * n : 2 * n + 4, :], b[2 * n : 2 * n + 4, :]),
                    jnp.where(first, b[2 * n : 2 * n + 4, :], a[2 * n : 2 * n + 4, :]),
                ],
                axis=0,
            )

        def copy_v(d, sl):
            ref = packs.at[sl]
            return remote(ref, ref, sw.at[d], rw.at[d], nextdev(d))

        def through(d):
            return slice(0, z + 1) if d == 0 else slice(z, nz)

        def vec_chain(d):
            if poses[d] > 0:
                copy_v(d, behind(d)).wait_recv()
            if poses[d] < nz - 1:
                copy_v(d, through(d)).start()

        def vec_close():
            total = packs[0, 0 : 2 * n, :]
            for t in range(1, nz):
                total = total + packs[t, 0 : 2 * n, :]
            for t in range(nz):
                held = packs[t, 2 * n : 2 * n + 8, :]
                for j in range(2):
                    for i in range(4):
                        at = i * n + 2 * t + j
                        hold_s[at : at + 1, :] = held[4 * j + i : 4 * j + i + 1, :]
            stepped, state = update(total, hold_s[0 : 2 * n, :], hold_s[2 * n : 4 * n, :], rate)
            cn[...] = stepped[0:n].astype(jnp.bfloat16)
            cb[...] = stepped[n : 2 * n].astype(jnp.bfloat16)
            step_s[...] = stepped
            state_s[...] = state

        at_sum = LAG_PAIR
        at_spread = LAG_PAIR + LAG_SUM * (nz - 1)
        side_sum = LAG_SUM * far
        side_spread = LAG_SUM * (nz - 1) + 2 * LAG_SIDE
        plan = [(0, lambda u: copy_a(u).start())]
        for d in range(2):
            if poses[d] > 0:
                plan.append((at_spread + LAG_GATHER * poses[d], functools.partial(relay_y, d=d)))
        plan.append((at_spread + LAG_GATHER * far, last_y))
        for d in range(2):
            if poses[d] > 0:
                plan.append((side_spread + LAG_GATHER * poses[d], functools.partial(relay_z, d=d)))
        plan.append((side_sum + 2 * LAG_SIDE, spread_z))
        for d in range(2):
            plan.append((LAG_SUM * poses[d], functools.partial(chain_z, d=d)))
        plan.append((side_sum, cross_z))
        plan.append((at_sum, pair_y))
        for d in range(2):
            plan.append((at_sum + LAG_SUM * poses[d], functools.partial(chain_y, d=d)))
        plan.append((at_sum + LAG_SUM * far, close_y))
        plan.append((side_sum + LAG_SIDE, close_z))
        plan.append((-1, encode_a))
        slots = units + max(lag for lag, _ in plan)
        vec_at = 2 + LAG_VECTOR
        extra = [(2, vec_send), (vec_at, vec_pair)]
        extra += [(vec_at + LAG_VECTOR * poses[d], functools.partial(vec_chain, d)) for d in range(2)]
        extra.append((vec_at + LAG_VECTOR * nz, vec_close))
        first_close = min(at_sum + LAG_SUM * far, side_sum + LAG_SIDE)

        def slot(s, carry):
            @pl.when(s == first_close)
            def _():
                for p in params:
                    p.wait()

            for lag, task in plan:
                u = s - lag

                @pl.when(jnp.logical_and(u >= 0, u < units))
                def _():
                    task(u)

            for when, step in extra:
                pl.when(s == when)(step)

            return carry

        lax.fori_loop(0, slots, slot, 0)

        remote(a_s, a_r, sa.at[0], ra.at[0], other).wait_send()
        for d in range(2):
            if poses[d] < nz - 1:
                copy_c(slice(None), d, beyond(d)).wait_send()
                copy_z(slice(None), d, beyond(d)).wait_send()
                ref = gy.at[:, z, y]
                remote(ref, ref, so.at[d], ro.at[d, 0], other).wait_send()
                ref = gz.at[:, z]
                remote(ref, ref, sp.at[d], rp.at[d, 0], other).wait_send()
                if poses[d] > 0:
                    ref = gy.at[:, behind(d), y]
                    remote(ref, ref, st.at[d], rt.at[d, 0], other).wait_send()
                    ref = gz.at[:, behind(d)]
                    remote(ref, ref, sq.at[d], rq.at[d, 0], other).wait_send()
                copy_v(d, through(d)).wait_send()
        remote(y_s, y_r, sy.at[0], ry.at[0], other).wait_send()
        ref = gz.at[:, z, y]
        remote(ref, ref, sg.at[0], rg.at[0], other).wait_send()
        remote(mine, theirs, sv.at[0], rv.at[0], other).wait_send()
        ref = gy.at[:, :, y]
        remote(ref, ref, sf.at[0], rf.at[0], other).wait_send()
        ref = gy.at[:, :, 1 - y]
        remote(ref, ref, sf.at[0], rf.at[0], other).wait_recv()

    for z in range(nz):
        pl.when(row == z)(functools.partial(run, z))


def leave(
    n, gy, gz, ou, od, qu, qd, cn, cb, step_s, state_s,
    cu, cd, tu, td, vu, vd, xcn, xcb, tn, tb, vn, vb, sem,
):
    me = lax.axis_index("replica")
    tiles, nz, _, halves, part_y, wide = gy.shape
    tiles_up = cu.shape[4] // wide
    size = cu.shape[3]
    pairs = []
    for ref, lo, hi in ((gy, 0, part_y), (gz, part_y, size)):
        for k in range(tiles_up):
            pairs.append((ref.at[k], cu.at[:, :, :, lo:hi, k * wide : (k + 1) * wide]))
        for b in range(n):
            pairs.append((ref.at[tiles_up:tiles, b // 2, b % 2], cd.at[:, :, lo:hi, b * wide : (b + 1) * wide]))
    pairs += [(ou, tu), (od, td), (qu, vu), (qd, vd), (cn, xcn), (cb, xcb)]
    pairs += [(step_s.at[pl.ds(me, 1), :], tn), (step_s.at[pl.ds(me + n, 1), :], tb)]
    pairs += [(state_s.at[pl.ds(me, 1), :], vn), (state_s.at[pl.ds(me + n, 1), :], vb)]
    copies = [pltpu.make_async_copy(a, b, sem.at[i]) for i, (a, b) in enumerate(pairs)]
    for c in copies:
        c.start()
    for c in copies:
        c.wait()


def fused(
    n, partial_up, partial_down, partial_norm, partial_bias, master_up, master_down,
    master_norm, master_bias, memory_up, memory_down, memory_norm, memory_bias,
):
    H = HALVES
    nz = n // 2
    hb, w = master_up.shape
    rows, wide = master_down.shape
    size, part_y, part_z = shares(hb)
    tiles_up, tiles_down = w // wide, rows // hb
    tiles = tiles_up + tiles_down
    units = tiles * H
    f32, b16 = jnp.float32, jnp.bfloat16
    line = lambda a: a.reshape(1, -1)
    operands = (
        partial_up[0].reshape(n, hb, w), partial_down[0].reshape(tiles_down, hb, n * wide),
        master_up, master_down, memory_up, memory_down,
        partial_norm.reshape(n, -1), partial_bias.reshape(n, -1),
        line(master_norm), line(master_bias), line(memory_norm), line(memory_bias),
    )
    S = jax.ShapeDtypeStruct
    shapes = (
        S((nz, 2, H, size, w), b16), S((tiles_down, H, size, n * wide), b16),
        S((hb, w), f32), S((rows, wide), f32), S((hb, w), f32), S((rows, wide), f32),
        S((n, wide), b16), S((n, wide), b16),
        S((1, wide), f32), S((1, wide), f32), S((1, wide), f32), S((1, wide), f32),
    )
    hbm = pl.BlockSpec(memory_space=pltpu.HBM)
    vm = pl.BlockSpec(memory_space=pltpu.VMEM)
    D = pltpu.SemaphoreType.DMA
    V = pltpu.VMEM
    one, two, each, both = D((1,)), D((2,)), D((units,)), D((2, units))
    held = pl.pallas_call(
        functools.partial(kernel, n),
        out_shape=(
            S((tiles, nz, 2, H, part_y, wide), b16), S((tiles, nz, 2, H, part_z, wide), b16),
            S((hb, w), f32), S((rows, wide), f32), S((hb, w), f32), S((rows, wide), f32),
            S((n, wide), b16), S((n, wide), b16), S((2 * n, wide), f32), S((2 * n, wide), f32),
        ),
        in_specs=[hbm] * 12,
        out_specs=[vm] * 10,
        scratch_shapes=[
            V((tiles, n, hb, wide), f32),
            V((hb, w), f32), V((rows, wide), f32), V((hb, w), f32), V((rows, wide), f32),
            *[V((units, nz, part_y, wide), b16)] * 6,
            *[V((units, nz, 2, part_z, wide), b16)] * 4,
            *[V((units, part_z, wide), b16)] * 2,
            V((2 * n + 8, wide), f32), V((2 * n + 8, wide), f32), V((nz, 2 * n + 8, wide), f32), V((4 * n, wide), f32),
            D((tiles_up,)), D((n,)), D((4,)), D((6,)),
            one, each, two, both, two, both, one, each, two, both, two, both,
            one, one, one, each, two, both, two, both, one, one, two, two,
        ],
        compiler_params=pltpu.CompilerParams(
            collective_id=0, has_side_effects=True, vmem_limit_bytes=28 * 1024 * 1024
        ),
    )(*[pltpu.with_memory_space_constraint(a, pltpu.HBM) for a in operands])
    cu, cd, tu, td, vu, vd, cn, cb, tn, tb, vn, vb = pl.pallas_call(
        functools.partial(leave, n),
        out_shape=shapes,
        in_specs=[vm] * 10,
        out_specs=[hbm] * 12,
        scratch_shapes=[D((2 * (tiles_up + n) + 10,))],
        compiler_params=pltpu.CompilerParams(vmem_limit_bytes=4 * 1024 * 1024),
    )(*held)
    flat = lambda a: a.reshape(-1)
    return (
        cu.reshape(n * hb, w), cd.reshape(rows, n * wide), flat(cn), flat(cb),
        tu, td, flat(tn), flat(tb), vu, vd, flat(vn), flat(vb),
    )


def on_device(*args):
    n = lax.axis_size("replica")
    (hb, w), (rows, wide) = args[4].shape, args[5].shape
    fits = n % 8 == 0 and n < 16 and wide == 128 and args[6].shape[0] == wide and args[7].shape[0] == wide
    fits = fits and hb % (32 * HALVES) == 0 and rows % hb == 0 and w % wide == 0
    return fused(n, *args) if fits else plain(*args)


def solution(mesh):
    in_specs = (
        P("replica", None, "model"),
        P("replica", "model", None),
        P("replica", None),
        P("replica", None),
        P("replica", "model"),
        P("model", "replica"),
        P("replica"),
        P("replica"),
        P("replica", "model"),
        P("model", "replica"),
        P("replica"),
        P("replica"),
    )
    out_specs = (
        P(None, "model"),
        P("model", None),
        P(),
        P(),
        P("replica", "model"),
        P("model", "replica"),
        P("replica"),
        P("replica"),
        P("replica", "model"),
        P("model", "replica"),
        P("replica"),
        P("replica"),
    )
    return jax.shard_map(
        on_device, mesh=mesh, in_specs=in_specs, out_specs=out_specs, check_vma=False
    )
```

time: 107 us -> 98.8 us (0.923)
  Pallas kernels: 106 us -> 98 us
    pallas_call x1, Pallas kernels: 103 us -> 95 us  [fused(): pl.pallas_call(functools.partial(kernel, n), out_shape=(S((tiles, nz, 2,...]
where the time goes in v1:
time: 98.8 us; the launch traced here: 98.7 us
  Pallas kernels  98 us (99%)
    pallas_call x1, Pallas kernels, fused(): pl.pallas_call(functools.partial(kernel, n), out_shape=(S((tiles, nz, 2,...  95 us
    pallas_call x1, Pallas kernels, fused(): pl.pallas_call(functools.partial(leave, n), out_shape=shapes, in_specs=[v...  3.04 us

profile of v1, /device:TPU:0, one launch (start us, length us, event | category | flops | bytes accessed | tf_op | source)
XLA Modules:
  0.0 98.7 jit_solution(3163748002598546413)
XLA Ops:
  0.6 95.0 %shard_map.211 = (bf16[16,4,2,2,40,128]{5,4,3,2,1,0:T(8,128)(2,1)S(1)}, bf16[16,4,2,2,24,128]{5,4,3,2,1,0:T(8,128)(2,1)S(1)}, f32[128,1024]{1,0:T(8,128)S(1)}, f...) custom-call(f32[8,128,1024]{2,1,0:T(8,128)} %bitcast.16, ...), custom_call_target="tpu_custom_call" | custom-call | tf_op jit(solution)/shard_map/pallas_call | solution.py:570
  95.6 3.0 %shard_map.212 = (bf16[4,2,2,64,1024]{4,3,2,1,0:T(8,128)(2,1)}, bf16[8,2,64,1024]{3,2,1,0:T(8,128)(2,1)}, f32[128,1024]{1,0:T(8,128)}, f32[1024,128]{1,0:T(8,128...) custom-call(bf16[16,4,2,2,40,128]{5,4,3,2,1,0:T(8,128)(2,1)S(1)} %ge, ...), custom_call_target="tpu_custom_call" | custom-call | tf_op jit(solution)/shard_map/pallas_call | solution.py:594
